TPU v7x, 32 devices: a whole 2x2x4 slice. The times are simulated.
32 devices in a mesh: row: 4 (over y, core), col: 8 (over z, x).
Axes of the slice: x: 2, y: 2, z: 4, core: 2. Of those that a mesh axis runs over, the one named last changes fastest.
Arguments:
- inner_base: bfloat16 [4, 1, 2, 4096, 14336], P(None, None, None, 'row', 'col'), may hold values from -250 to 250
- inner_left: bfloat16 [4, 1, 2, 4096, 16], P(None, None, None, ('row', 'col')), may hold values from -6 to 6
- inner_right: bfloat16 [4, 1, 2, 16, 14336], P(None, None, None, 'row', 'col'), may hold values from -12 to 12
- inner_mag: float32 [4, 1, 2, 14336], P(None, None, None, 'col'), may hold values from 512 to 2048
- outer_base: bfloat16 [4, 1, 14336, 4096], P(None, None, 'row', 'col'), may hold values from -250 to 250
- outer_left: bfloat16 [4, 1, 14336, 16], P(None, None, ('row', 'col')), may hold values from -6 to 6
- outer_right: bfloat16 [4, 1, 16, 4096], P(None, None, 'row', 'col'), may hold values from -12 to 12
- outer_mag: float32 [4, 1, 4096], P(None, None, 'col'), may hold values from 1792 to 7168
Outputs:
- inner_merged: bfloat16 [4, 1, 2, 4096, 14336], P(None, None, None, 'row', 'col')
- outer_merged: bfloat16 [4, 1, 14336, 4096], P(None, None, 'row', 'col')
All inputs are finite; a program needn't handle non-finite values.
Results may differ from a plain program's by a relative error of at most 0.001.
Values may be sent and summed in bfloat16 or wider, within the bound.
A program may use at most 256 MiB of HBM per device.

v0:
```python
import jax
import jax.numpy as jnp
from jax import lax
from jax.sharding import PartitionSpec as P

epsilon = 1e-06


def combine_tile(base, left, right):
    delta = jnp.einsum("...ik,...kj->...ij", left, right, preferred_element_type=jnp.float32)
    return base.astype(jnp.float32) + delta


def merge_layer(
    inner_base, outer_base, inner_mag, outer_mag, inner_left, outer_left, inner_right, outer_right
):
    inner_full = combine_tile(inner_base, inner_left, inner_right)
    outer_full = combine_tile(outer_base, outer_left, outer_right)
    inner_squares = jnp.sum(inner_full * inner_full, axis=-2)
    outer_squares = jnp.sum(outer_full * outer_full, axis=-2)
    inner_totals, outer_totals = lax.psum((inner_squares, outer_squares), "row")
    inner_scale = lax.rsqrt(inner_totals + epsilon)
    outer_scale = lax.rsqrt(outer_totals + epsilon)
    inner_factor = inner_mag * inner_scale
    outer_factor = outer_mag * outer_scale
    inner_merged = (inner_factor[..., None, :] * inner_full).astype(jnp.bfloat16)
    outer_merged = (outer_factor[..., None, :] * outer_full).astype(jnp.bfloat16)
    return (inner_merged, outer_merged)


def shards(
    inner_base, inner_left, inner_right, inner_mag, outer_base, outer_left, outer_right, outer_mag
):
    layer_count = inner_base.shape[0]
    inner_outputs = []
    outer_outputs = []
    inner_rows, outer_rows = (
        lax.all_gather(inner_left, "col", axis=3, tiled=True),
        lax.all_gather(outer_left, "col", axis=2, tiled=True),
    )
    inner_ranks, outer_ranks = (
        lax.all_gather(inner_right, "row", axis=3, tiled=True),
        lax.all_gather(outer_right, "row", axis=2, tiled=True),
    )
    for layer_index in range(layer_count):
        inner_merged, outer_merged = merge_layer(
            inner_base[layer_index],
            outer_base[layer_index],
            inner_mag[layer_index],
            outer_mag[layer_index],
            inner_rows[layer_index],
            outer_rows[layer_index],
            inner_ranks[layer_index],
            outer_ranks[layer_index],
        )
        inner_outputs.append(inner_merged)
        outer_outputs.append(outer_merged)
    return (jnp.stack(inner_outputs), jnp.stack(outer_outputs))


def solution(mesh):
    in_specs = (
        P(None, None, None, "row", "col"),
        P(None, None, None, ("row", "col"), None),
        P(None, None, None, "row", "col"),
        P(None, None, None, "col"),
        P(None, None, "row", "col"),
        P(None, None, ("row", "col"), None),
        P(None, None, "row", "col"),
        P(None, None, "col"),
    )
    out_specs = (P(None, None, None, "row", "col"), P(None, None, "row", "col"))
    return jax.shard_map(shards, mesh=mesh, in_specs=in_specs, out_specs=out_specs, check_vma=False)
```

profile of v0, /device:TPU:1, one launch (start us, length us, event | category | flops | bytes accessed | tf_op | source)
XLA Modules:
  0.0 345.2 jit_solution(11478895397710720571)
XLA Ops:
  7.2 0.0 all-reduce.3.cloned.1.call-start
  7.2 0.9 copy.17
  8.2 8.2 %all_gather.13 = bf16[4,1,2,16,1792]{4,0,2,1,3:T(4,128)(2,1)S(1)} all-gather(bf16[4,1,2,4,1792]{4,0,2,1,3:T(4,128)(2,1)S(1)} %copy.17), channel_id=1, replica_groups=mesh['row'=4,'col'=8] {'row'}, dimensions={3}, use_global_device_ids=true | all-gather | bytes 573440 | tf_op jit(solution)/shard_map/all_gather | solution.py:42
  16.3 0.7 fusion.21
  17.0 22.4 %all_gather.12 = bf16[4,1,2,1024,16]{3,4,2,1,0:T(8,128)(2,1)S(1)} all-gather(bf16[4,1,2,128,16]{3,4,2,1,0:T(8,128)(2,1)} %param.9), channel_id=1, replica_groups=mesh['row'=4,'col'=8] {'col'}, dimensions={3}, use_global_device_ids=true | all-gather | bytes 294912 | tf_op jit(solution)/shard_map/all_gather | solution.py:38
  39.4 7.6 %fusion.10 = f32[2,1024,1792]{2,1,0:T(8,128)} fusion(bf16[1,1,2,16,1792]{4,0,2,1,3:T(2,128)(2,1)S(1)} %get-tuple-element.23, bf16[4,1,2,1024,16]{3,4,2,1,0:T(8,128)(2,1)S(1)} %all_gather.12), kind=kOutput, calls=%fused_computation.39 | convolution fusion | flops 117440512 | bytes 14974976 | tf_op jit(solution)/shard_map/...ik,...kj->...ij/dot_general | solution.py:10
  47.0 7.3 %fusion.8 = f32[2,1024,1792]{2,1,0:T(8,128)} fusion(bf16[1,1,2,16,1792]{4,0,2,1,3:T(2,128)(2,1)S(1)} %get-tuple-element.25, bf16[4,1,2,1024,16]{3,4,2,1,0:T(8,128)(2,1)S(1)} %all_gather.12), kind=kOutput, calls=%fused_computation.35 | convolution fusion | flops 117440512 | bytes 14974976 | tf_op jit(solution)/shard_map/...ik,...kj->...ij/dot_general | solution.py:10
  54.3 0.0 copy-start
  54.3 7.3 %fusion.9 = f32[2,1024,1792]{2,1,0:T(8,128)} fusion(bf16[1,1,2,16,1792]{4,0,2,1,3:T(2,128)(2,1)S(1)} %get-tuple-element.22, bf16[4,1,2,1024,16]{3,4,2,1,0:T(8,128)(2,1)S(1)} %all_gather.12), kind=kOutput, calls=%fused_computation.37 | convolution fusion | flops 117440512 | bytes 14974976 | tf_op jit(solution)/shard_map/...ik,...kj->...ij/dot_general | solution.py:10
  61.6 0.0 copy-done
  61.6 0.3 copy.22
  61.9 73.3 %all_gather.14 = bf16[4,1,3584,16]{3,0,1,2:T(4,128)(2,1)S(1)} all-gather(bf16[4,1,448,16]{3,0,1,2:T(4,128)(2,1)S(1)} %copy.22), channel_id=1, replica_groups=mesh['row'=4,'col'=8] {'col'}, dimensions={2}, use_global_device_ids=true | all-gather | bytes 516096 | tf_op jit(solution)/shard_map/all_gather | solution.py:39
  135.1 0.0 copy-start.2
  135.1 6.7 %fusion.20 = (bf16[1,1,3584,16]{3,0,1,2:T(2,128)(2,1)}, bf16[1,1,3584,16]{3,0,1,2:T(2,128)(2,1)}, bf16[1,1,3584,16]{3,0,1,2:T(2,128)(2,1)}, bf16[1,1,3584,16]{3,0,1,2:T(2,128)(2,1)S(1)}) fusion(bf16[4,1,3584,16]{3,0,1,2:T(4,128)(2,1)S(1)} %all_gather.14), kind=kLoop, calls=%fused_computation.66 | loop fusion | bytes 917504 | tf_op jit(solution)/shard_map/slice | solution.py:52
  141.8 3.5 %copy.36 = bf16[1,1,3584,16]{2,3,1,0:T(8,128)(2,1)S(1)} copy(bf16[1,1,3584,16]{3,0,1,2:T(2,128)(2,1)} %get-tuple-element.18) | data formatting | bytes 229376
  145.3 0.0 copy-done.2
  145.4 6.1 %all_gather.15 = bf16[4,1,16,512]{3,0,1,2:T(4,128)(2,1)S(1)} all-gather(bf16[4,1,4,512]{3,0,1,2:T(4,128)(2,1)S(1)} %copy.24), channel_id=1, replica_groups=mesh['row'=4,'col'=8] {'row'}, dimensions={2}, use_global_device_ids=true | all-gather | bytes 81920 | tf_op jit(solution)/shard_map/all_gather | solution.py:43
  151.5 0.1 fusion.22
  151.6 3.7 %copy.38 = bf16[1,1,3584,16]{2,3,1,0:T(8,128)(2,1)S(1)} copy(bf16[1,1,3584,16]{3,0,1,2:T(2,128)(2,1)} %get-tuple-element.20) | data formatting | bytes 229376
  155.3 3.5 %copy.40 = bf16[1,1,3584,16]{2,3,1,0:T(8,128)(2,1)S(1)} copy(bf16[1,1,3584,16]{3,0,1,2:T(2,128)(2,1)} %get-tuple-element.19) | data formatting | bytes 229376
  158.8 1.8 copy.42
  160.7 6.7 %multiply_reduce_fusion.7 = (f32[512]{0:T(512)}, f32[3584,512]{1,0:T(8,128)}) fusion(bf16[1,1,16,512]{3,0,1,2:T(2,128)(2,1)S(1)} %get-tuple-element.26, bf16[1,1,3584,16]{2,3,1,0:T(8,128)(2,1)S(1)} %copy.36, bf16[4,1,3584,512]{3,2,1,0:T(8,128)(2,1)} %param.12), kind=kOutput, calls=%fused_computation.29 | convolution fusion | flops 66059776 | bytes 11143168 | tf_op jit(solution)/shard_map/...ik,...kj->...ij/dot_general | solution.py:10
  167.3 6.8 %multiply_reduce_fusion.6 = (f32[512]{0:T(512)}, f32[3584,512]{1,0:T(8,128)}) fusion(bf16[1,1,16,512]{3,0,1,2:T(2,128)(2,1)S(1)} %get-tuple-element.28, bf16[1,1,3584,16]{2,3,1,0:T(8,128)(2,1)S(1)} %copy.38, bf16[4,1,3584,512]{3,2,1,0:T(8,128)(2,1)} %param.12), kind=kOutput, calls=%fused_computation.27 | convolution fusion | flops 66059776 | bytes 11143168 | tf_op jit(solution)/shard_map/...ik,...kj->...ij/dot_general | solution.py:10
  174.1 6.8 %multiply_reduce_fusion.5 = (f32[512]{0:T(512)}, f32[3584,512]{1,0:T(8,128)}) fusion(bf16[1,1,16,512]{3,0,1,2:T(2,128)(2,1)S(1)} %get-tuple-element.27, bf16[1,1,3584,16]{2,3,1,0:T(8,128)(2,1)S(1)} %copy.40, bf16[4,1,3584,512]{3,2,1,0:T(8,128)(2,1)} %param.12), kind=kOutput, calls=%fused_computation.25 | convolution fusion | flops 66059776 | bytes 11143168 | tf_op jit(solution)/shard_map/...ik,...kj->...ij/dot_general | solution.py:10
  180.9 6.8 %multiply_reduce_fusion.4 = (f32[512]{0:T(512)}, f32[3584,512]{1,0:T(8,128)}) fusion(bf16[1,1,16,512]{3,0,1,2:T(2,128)(2,1)S(1)} %get-tuple-element.29, bf16[1,1,3584,16]{2,3,1,0:T(8,128)(2,1)S(1)} %copy.42, bf16[4,1,3584,512]{3,2,1,0:T(8,128)(2,1)} %param.12), kind=kOutput, calls=%fused_computation.23 | convolution fusion | flops 66059776 | bytes 11143168 | tf_op jit(solution)/shard_map/...ik,...kj->...ij/dot_general | solution.py:10
  187.7 0.0 copy-start.7
  187.7 30.8 %multiply_reduce_fusion.3 = (f32[2,1792]{1,0:T(2,128)}, f32[2,1792]{1,0:T(2,128)}, f32[2,1792]{1,0:T(2,128)}, f32[2,1792]{1,0:T(2,128)}, f32[2,1024,1792]{2,1,0:T(8,128)}) fusion(bf16[4,1,2,1024,1792]{4,3,2,1,0:T(8,128)(2,1)} %param.8, f32[2,1024,1792]{2,1,0:T(8,128)} %fusion.10, f32[2,1024,1792]{2,1,0:T(8,128)} %fusion.8, f32[2,1024,1792]{2,1,0:T(8,128)} %fusion.9, ...), kind=kOutput, calls=%fused_computation.13 | convolution fusion | flops 176146432 | bytes 88432640 | tf_op jit(solution)/shard_map/...ik,...kj->...ij/dot_general | solution.py:10
  218.5 0.0 all-reduce.3.cloned.1.call-update
  218.5 28.6 %all-reduce.3.cloned.1.call-done = (f32[1,2,1792]{2,1,0:T(2,128)}, f32[1,2,1792]{2,1,0:T(2,128)}, f32[1,2,1792]{2,1,0:T(2,128)}, f32[1,2,1792]{2,1,0:T(2,128)}, ...) async-done(((f32[1,2,1792]{2,1,0:T(2,128)}, f32[1,2,1792]{2,1,0:T(2,128)}, f32[1,2,1792]{2,1,0:T(2,128)}, f32[1,2,1792]{2,1,0:T(2,128)}, ...) | async-done | bytes 65552 | tf_op jit(solution)/shard_map/psum | solution.py:21
  247.1 0.0 copy-done.7
  247.1 0.7 bitcast_multiply_fusion.7
  247.8 9.1 %fusion.4 = (bf16[1,1,3584,512]{3,2,1,0:T(8,128)(2,1)S(1)}, bf16[1,1,3584,512]{3,2,1,0:T(8,128)(2,1)}) fusion(f32[3584,512]{1,0:T(8,128)} %get-tuple-element.46, f32[512]{0:T(512)S(1)} %bitcast.166, f32[3584,512]{1,0:T(8,128)} %get-tuple-element.44, f32[512]{0:T(512)S(1)} %bitcast.167), kind=kLoop, calls=%fused_computation.30 | loop fusion | flops 7340032 | bytes 22024192 | tf_op jit(solution)/shard_map/stack | solution.py:58
  256.9 10.2 %fusion.6 = (bf16[1,1,3584,512]{3,2,1,0:T(8,128)(2,1)}, bf16[1,1,3584,512]{3,2,1,0:T(8,128)(2,1)}) fusion(f32[3584,512]{1,0:T(8,128)} %get-tuple-element.42, f32[512]{0:T(512)S(1)} %bitcast.165, f32[3584,512]{1,0:T(8,128)} %get-tuple-element.40, f32[512]{0:T(512)S(1)} %bitcast.164), kind=kLoop, calls=%fused_computation.32 | loop fusion | flops 7340032 | bytes 22024192 | tf_op jit(solution)/shard_map/stack | solution.py:58
  267.1 0.0 copy-start.1
  267.1 0.0 copy-start.3
  267.1 0.0 copy-start.4
  267.1 0.0 copy-start.5
  267.1 0.0 copy-start.6
  267.1 11.8 %pad_maximum_fusion.1 = bf16[4,1,3584,512]{3,2,1,0:T(8,128)(2,1)} fusion(bf16[1,1,3584,512]{3,2,1,0:T(8,128)(2,1)} %get-tuple-element.50, bf16[1,1,3584,512]{3,2,1,0:T(8,128)(2,1)} %get-tuple-element.49, bf16[1,1,3584,512]{3,2,1,0:T(8,128)(2,1)} %get-tuple-element.48, bf16[1,1,3584,512]{3,2,1,0:T(8,128)(2,1)S(1)} %get-tuple-element.47), kind=kLoop, calls=%fused_computation.1 | loop fusion | flops 22020096 | bytes 29360128 | tf_op jit(solution)/shard_map/stack | solution.py:58
  278.9 0.0 copy-done.1
  278.9 0.0 copy-done.3
  278.9 0.0 copy-done.4
  278.9 0.0 copy-done.5
  279.0 0.0 copy-done.6
  279.0 38.7 %fusion = (bf16[1,1,2,1024,1792]{4,3,2,1,0:T(8,128)(2,1)}, bf16[1,1,2,1024,1792]{4,3,2,1,0:T(8,128)(2,1)}, bf16[1,1,2,1024,1792]{4,3,2,1,0:T(8,128)(2,1)}, bf16[1,1,2,1024,1792]{4,3,2,1,0:T(8,128)(2,1)}) fusion(f32[2,1024,1792]{2,1,0:T(8,128)} %get-tuple-element.38, f32[2,1792]{1,0:T(2,128)S(1)} %get-tuple-element.30, ...), kind=kLoop, calls=%fused_computation.14 | loop fusion | flops 58720256 | bytes 117497856 | tf_op jit(solution)/shard_map/stack | solution.py:58
  317.7 20.6 %pad_maximum_fusion = bf16[4,1,2,1024,1792]{4,3,2,1,0:T(8,128)(2,1)} fusion(bf16[1,1,2,1024,1792]{4,3,2,1,0:T(8,128)(2,1)} %get-tuple-element.15, bf16[1,1,2,1024,1792]{4,3,2,1,0:T(8,128)(2,1)} %get-tuple-element.17, bf16[1,1,2,1024,1792]{4,3,2,1,0:T(8,128)(2,1)} %get-tuple-element.16, bf16[1,1,2,1024,1792]{4,3,2,1,0:T(8,128)(2,1)} %get-tuple-element.14), kind=kLoop, calls=%fused_computation | loop fusion | flops 44040192 | bytes 58720256 | tf_op jit(solution)/shard_map/stack | solution.py:58
  (2 shorter events, 0.1 us)
Async XLA Ops:
  7.2 239.9 %all-reduce.3.cloned.1.call-start = ((), (), s32[]{:S(2)}) async-start(), calls=%async_computation | async-start | bytes 131072 | tf_op jit(solution)/shard_map/psum | solution.py:21
  54.3 7.3 %copy-start = (bf16[4,1,448,16]{2,3,1,0:T(8,128)(2,1)S(1)}, bf16[4,1,448,16]{2,3,1,0:T(8,128)(2,1)}, u32[]{:S(2)}) copy-start(bf16[4,1,448,16]{2,3,1,0:T(8,128)(2,1)} %param.13) | copy-start | bytes 172036
  135.1 10.2 %copy-start.2 = (bf16[4,1,4,512]{3,2,1,0:T(4,128)(2,1)S(1)}, bf16[4,1,4,512]{3,2,1,0:T(4,128)(2,1)}, u32[]{:S(2)}) copy-start(bf16[4,1,4,512]{3,2,1,0:T(4,128)(2,1)} %param.14) | copy-start | bytes 49156
  187.7 59.4 %copy-start.7 = (f32[4,1,512]{2,1,0:T(1,128)S(1)}, f32[4,1,512]{2,1,0:T(1,128)}, u32[]{:S(2)}) copy-start(f32[4,1,512]{2,1,0:T(1,128)} %param.15) | copy-start | bytes 24580
  267.1 11.8 %copy-start.1 = (f32[4,1,2,1792]{3,2,1,0:T(2,128)S(1)}, f32[4,1,2,1792]{3,2,1,0:T(2,128)}, u32[]{:S(2)}) copy-start(f32[4,1,2,1792]{3,2,1,0:T(2,128)} %param.11) | copy-start | bytes 172036
  267.1 11.8 %copy-start.3 = (f32[1,2,1792]{2,1,0:T(2,128)S(1)}, f32[1,2,1792]{2,1,0:T(2,128)}, u32[]{:S(2)}) copy-start(f32[1,2,1792]{2,1,0:T(2,128)} %get-tuple-element.6) | copy-start | bytes 43012
  267.1 11.8 %copy-start.4 = (f32[1,2,1792]{2,1,0:T(2,128)S(1)}, f32[1,2,1792]{2,1,0:T(2,128)}, u32[]{:S(2)}) copy-start(f32[1,2,1792]{2,1,0:T(2,128)} %get-tuple-element.7) | copy-start | bytes 43012
  267.1 11.8 %copy-start.5 = (f32[1,2,1792]{2,1,0:T(2,128)S(1)}, f32[1,2,1792]{2,1,0:T(2,128)}, u32[]{:S(2)}) copy-start(f32[1,2,1792]{2,1,0:T(2,128)} %get-tuple-element.8) | copy-start | bytes 43012
  267.1 11.8 %copy-start.6 = (f32[1,2,1792]{2,1,0:T(2,128)S(1)}, f32[1,2,1792]{2,1,0:T(2,128)}, u32[]{:S(2)}) copy-start(f32[1,2,1792]{2,1,0:T(2,128)} %get-tuple-element.9) | copy-start | bytes 43012
Sparse Core Ops, SparseCore 0:
  218.6 28.4 all-reduce.2
where the time goes:
time: 348 us; the launch traced here: 345 us
  blocking collectives  110 us (32%)
  other arithmetic  91.3 us (26%)
  matrix products  80 us (23%)
  waiting for transfers between devices  28.6 us (8%)
  local copies, waits for them, and re-layouts  21.2 us (6%)
  between operations  14.2 us (4%)
    another operation x5, other arithmetic, shards(): return (jnp.stack(inner_outputs), jnp.stack(outer_outputs))  90.5 us
    dot_general x8, matrix products, combine_tile(): jnp.einsum('...ik,...kj->...ij', left, right, preferred_element_type=jnp....  80 us
    all_gather x1, blocking collectives, shards(): lax.all_gather(outer_left, 'col', axis=2, tiled=True)  73.3 us
    psum x1, waiting for transfers between devices, merge_layer(): inner_totals, outer_totals = lax.psum((inner_squares, outer_squares), 'row')  28.6 us
    all_gather x1, blocking collectives, shards(): lax.all_gather(inner_left, 'col', axis=3, tiled=True)  22.4 us
    unnamed x23, local copies, waits for them, and re-layouts  13.8 us
    all_gather x1, blocking collectives, shards(): lax.all_gather(inner_right, 'row', axis=3, tiled=True)  8.17 us
  transfers between devices with their start and end apart: 1, of which 1 were waited for; matrix products, arithmetic and copies ran while one was open for 0% of the time, Pallas kernels for 0%

commit v1 on v0

v1 whole, which is shorter than its diff:
```python
import functools

import jax
import jax.numpy as jnp
from jax import lax
from jax.experimental import pallas as pl
from jax.experimental.pallas import tpu as pltpu
from jax.sharding import PartitionSpec as P

epsilon = 1e-06
MESH = pl.DeviceIdType.MESH
ANY = pl.BlockSpec(memory_space=pl.ANY)
VMEM = pl.BlockSpec(memory_space=pltpu.VMEM)
GRANT = 18 << 20
SLOTS, PIECES = 4, 4


def peers_of(axis, n):
    me = lax.axis_index(axis)
    low, high, half = lax.rem(me, 2), lax.div(me, 2), n // 2
    partner = me + 1 - 2 * low
    ahead = [lax.rem(high + k, half) * 2 + low for k in range(1, half)]
    behind = [lax.rem(high + half - k, half) * 2 + low for k in range(1, half)]
    return me, partner, ahead, behind


def remote(src, dst, send, recv, axis, target):
    return pltpu.make_async_remote_copy(
        src_ref=src, dst_ref=dst, send_sem=send, recv_sem=recv, device_id={axis: target}, device_id_type=MESH
    )


def gather_kernel(rows, cols, il, ol, ir, orr, ib, ob, gil, gol, gir, gor, vib, vob, local, loads, send, recv):
    barrier = pltpu.get_barrier_semaphore()
    places = {"row": peers_of("row", rows), "col": peers_of("col", cols)}
    greeted = 0
    for axis, (_, partner, ahead, _) in places.items():
        for other in [partner, *ahead]:
            pl.semaphore_signal(barrier, inc=1, device_id={axis: other}, device_id_type=MESH)
            greeted += 1
    pl.semaphore_wait(barrier, greeted)
    items = [("row", rows, ir, gir), ("col", cols, il, gil), ("row", rows, orr, gor), ("col", cols, ol, gol)]
    sends, forwards, slot = [], [], 0
    for number, (axis, n, src, dst) in enumerate(items):
        me, partner, ahead, behind = places[axis]
        mine = pltpu.make_async_copy(src, dst.at[me], local.at[number])
        mine.start()
        arrivals = []
        for k, other in enumerate(ahead):
            copy = remote(src, dst.at[me], send.at[slot], recv.at[slot], axis, other)
            copy.start()
            sends.append(copy)
            arrivals.append((slot, behind[k]))
            slot += 1
        copy = remote(src, dst.at[me], send.at[slot], recv.at[slot], axis, partner)
        copy.start()
        sends.append(copy)
        forwards.append((copy, mine))
        slot += 1
        items[number] = (axis, dst, partner, arrivals)
    bases = []
    for number, (src, dst) in enumerate(((ib, vib), (ob, vob))):
        for t in range(src.shape[0]):
            copy = pltpu.make_async_copy(src.at[t], dst.at[t], loads.at[len(bases)])
            copy.start()
            bases.append(copy)
    last = [f for f, _ in forwards]
    for axis, dst, partner, arrivals in items:
        for number, source in arrivals:
            remote(dst.at[source], dst.at[source], send.at[number], recv.at[number], axis, partner).wait_recv()
            copy = remote(dst.at[source], dst.at[source], send.at[slot], recv.at[slot], axis, partner)
            copy.start()
            sends.append(copy)
            last.append(copy)
            slot += 1
    for copy in last:
        copy.wait_recv()
    for copy in sends:
        copy.wait_send()
    for _, mine in forwards:
        mine.wait()
    for copy in bases:
        copy.wait()


def prepare(left, right, lt, r32, t, rank):
    pieces, _, _, piece = left.shape
    for c in range(pieces):
        lt[c * piece : (c + 1) * piece, :] = left[c, t].T
    for c in range(right.shape[0]):
        share = right.shape[2]
        r32[c * share : (c + 1) * share, :] = right[c, t].astype(jnp.float32)


def tiles(rows, cols):
    width = 256 if cols % 256 == 0 else 128 if cols % 128 == 0 else cols
    height = next(h for h in (256, 128, 64, 32, 16) if rows % h == 0)
    return height, width


def squares_weight(left, right, base, out, lt, r32, r16, acc):
    count, rows, cols = base.shape
    height, width = tiles(rows, cols)

    @pl.loop(0, count)
    def _(t):
        prepare(left, right, lt, r32, t, r32.shape[0])
        r16[...] = r32[...].astype(jnp.bfloat16)
        for j in range(cols // width):
            part = slice(j * width, (j + 1) * width)

            def add(i, total):
                span = pl.ds(pl.multiple_of(i * height, height), height)
                delta = jnp.dot(lt[span, :], r16[:, part], preferred_element_type=jnp.float32)
                full = base[t, span, part].astype(jnp.float32) + delta
                return total + jnp.sum((full * full).reshape(height // 8, 8, width), axis=0)

            total = lax.fori_loop(0, rows // height, add, jnp.zeros((8, width), jnp.float32))
            acc[:, part] = total
        out[t] = jnp.sum(acc[...], axis=0, keepdims=True)


def squares_kernel(gil, gol, gir, gor, vib, vob, sin, sout, lti, lto, r32i, r32o, r16i, r16o, acci, acco):
    squares_weight(gil, gir, vib, sin, lti, r32i, r16i, acci)
    squares_weight(gol, gor, vob, sout, lto, r32o, r16o, acco)


def factor_kernel(rows, sin, sout, min_, mout, fin, fout, hin, hout, send, recv):
    me = lax.axis_index("row")
    barrier = pltpu.get_barrier_semaphore()
    others = [lax.rem(me + k, rows) for k in range(1, rows)]
    for other in others:
        pl.semaphore_signal(barrier, inc=1, device_id={"row": other}, device_id_type=MESH)
    pl.semaphore_wait(barrier, rows - 1)
    copies = []
    for k, other in enumerate(others):
        for number, (src, held) in enumerate(((sin, hin), (sout, hout))):
            slot = 2 * k + number
            copy = remote(src, held.at[k], send.at[slot], recv.at[slot], "row", other)
            copy.start()
            copies.append(copy)
    for copy in copies:
        copy.wait()
    for src, held, mag, out in ((sin, hin, min_, fin), (sout, hout, mout, fout)):
        total = src[...]
        for k in range(rows - 1):
            total = total + held[k]
        scale = lax.rsqrt(total + epsilon)
        groups = mag.shape[1]
        for t in range(out.shape[0]):
            row = t % groups
            out[t] = mag[t // groups, row : row + 1, :] * scale[t]


def scale_weight(left, right, base, factor, out, lt, r32, r16, stage, sems):
    count, rows, cols = base.shape
    slots, chunk, _ = stage.shape
    pieces = rows // chunk
    height, width = tiles(chunk, cols)

    def store(step):
        slot = lax.rem(step, slots)
        span = pl.ds(pl.multiple_of(lax.rem(step, pieces) * chunk, chunk), chunk)
        return pltpu.make_async_copy(stage.at[slot], out.at[lax.div(step, pieces), span], sems.at[slot])

    @pl.loop(0, count)
    def _(t):
        prepare(left, right, lt, r32, t, r32.shape[0])
        r16[...] = r32[...].astype(jnp.bfloat16)

        @pl.loop(0, pieces)
        def _(p):
            step = t * pieces + p
            slot = lax.rem(step, slots)

            @pl.when(step >= slots)
            def _():
                store(step - slots).wait()

            for j in range(cols // width):
                part = slice(j * width, (j + 1) * width)
                scale = jnp.broadcast_to(factor[t, :, part], (8, width))

                def merge(i, carry):
                    span = pl.ds(pl.multiple_of(p * chunk + i * height, height), height)
                    delta = jnp.dot(lt[span, :], r16[:, part], preferred_element_type=jnp.float32)
                    full = base[t, span, part].astype(jnp.float32) + delta
                    merged = full.reshape(height // 8, 8, width) * scale[None]
                    local = pl.ds(pl.multiple_of(i * height, height), height)
                    stage[slot, local, part] = merged.reshape(height, width).astype(jnp.bfloat16)
                    return carry

                lax.fori_loop(0, chunk // height, merge, 0)
            store(step).start()

    return [store(step) for step in range(count * pieces - slots, count * pieces)]


def scale_kernel(
    gil, gol, gir, gor, vib, vob, fin, fout, oin, oout, lti, lto, r32i, r32o, r16i, r16o, stagei, stageo, semi, semo
):
    stores = scale_weight(gil, gir, vib, fin, oin, lti, r32i, r16i, stagei, semi)
    stores += scale_weight(gol, gor, vob, fout, oout, lto, r32o, r16o, stageo, semo)
    for copy in stores:
        copy.wait()


def pinned(arrays):
    return [pltpu.with_memory_space_constraint(a, pltpu.VMEM) for a in arrays]


def shards(rows, cols, inner_base, inner_left, inner_right, inner_mag, outer_base, outer_left, outer_right, outer_mag):
    rank = inner_left.shape[-1]
    ib = inner_base.reshape((-1, *inner_base.shape[-2:]))
    ob = outer_base.reshape((-1, *outer_base.shape[-2:]))
    il = jnp.swapaxes(inner_left, -1, -2).reshape((-1, rank, inner_left.shape[-2]))
    ol = jnp.swapaxes(outer_left, -1, -2).reshape((-1, rank, outer_left.shape[-2]))
    ir = inner_right.reshape((-1, *inner_right.shape[-2:]))
    orr = outer_right.reshape((-1, *outer_right.shape[-2:]))
    im = inner_mag.reshape((-1, *inner_mag.shape[-2:]))
    om = outer_mag.reshape((ob.shape[0], 1, -1))
    weights, bf16, f32 = ib.shape[0] + ob.shape[0], jnp.bfloat16, jnp.float32
    copies = 4 * (cols + rows)
    gathered = pl.pallas_call(
        functools.partial(gather_kernel, rows, cols),
        out_shape=[
            pltpu.VMEM((n, *a.shape), bf16) for n, a in ((cols, il), (cols, ol), (rows, ir), (rows, orr))
        ] + [pltpu.VMEM(a.shape, bf16) for a in (ib, ob)],
        in_specs=[ANY] * 6,
        out_specs=[VMEM] * 6,
        scratch_shapes=[
            pltpu.SemaphoreType.DMA((4,)),
            pltpu.SemaphoreType.DMA((weights,)),
            pltpu.SemaphoreType.DMA((copies,)),
            pltpu.SemaphoreType.DMA((copies,)),
        ],
        compiler_params=pltpu.CompilerParams(collective_id=0, has_side_effects=True, vmem_limit_bytes=GRANT),
        name="gather",
    )(il, ol, ir, orr, ib, ob)
    gathered = pinned(gathered)
    work = []
    for shape in ((ib.shape[1], rank), (ob.shape[1], rank)):
        work.append(pltpu.VMEM(shape, bf16))
    for kind in (f32, bf16):
        for base in (ib, ob):
            work.append(pltpu.VMEM((rank, base.shape[2]), kind))
    sums = pl.pallas_call(
        squares_kernel,
        out_shape=[pltpu.VMEM((a.shape[0], 1, a.shape[2]), f32) for a in (ib, ob)],
        in_specs=[VMEM] * 6,
        out_specs=[VMEM] * 2,
        scratch_shapes=work + [pltpu.VMEM((8, a.shape[2]), f32) for a in (ib, ob)],
        compiler_params=pltpu.CompilerParams(vmem_limit_bytes=GRANT),
        name="squares",
    )(*gathered)
    sums = pinned(sums)
    factors = pl.pallas_call(
        functools.partial(factor_kernel, rows),
        out_shape=[pltpu.VMEM(s.shape, f32) for s in sums],
        in_specs=[VMEM] * 4,
        out_specs=[VMEM] * 2,
        scratch_shapes=[pltpu.VMEM((rows - 1, *s.shape), f32) for s in sums]
        + [pltpu.SemaphoreType.DMA((2 * rows - 2,))] * 2,
        compiler_params=pltpu.CompilerParams(collective_id=1, has_side_effects=True, vmem_limit_bytes=GRANT),
        name="factor",
    )(*sums, im, om)
    inner, outer = pl.pallas_call(
        scale_kernel,
        out_shape=[jax.ShapeDtypeStruct(a.shape, bf16) for a in (ib, ob)],
        in_specs=[VMEM] * 8,
        out_specs=[ANY] * 2,
        scratch_shapes=work
        + [pltpu.VMEM((SLOTS, a.shape[1] // PIECES, a.shape[2]), bf16) for a in (ib, ob)]
        + [pltpu.SemaphoreType.DMA((SLOTS,))] * 2,
        compiler_params=pltpu.CompilerParams(vmem_limit_bytes=GRANT),
        name="scale",
    )(*gathered, *pinned(factors))
    return inner.reshape(inner_base.shape), outer.reshape(outer_base.shape)


def solution(mesh):
    in_specs = (
        P(None, None, None, "row", "col"),
        P(None, None, None, ("row", "col"), None),
        P(None, None, None, "row", "col"),
        P(None, None, None, "col"),
        P(None, None, "row", "col"),
        P(None, None, ("row", "col"), None),
        P(None, None, "row", "col"),
        P(None, None, "col"),
    )
    out_specs = (P(None, None, None, "row", "col"), P(None, None, "row", "col"))
    body = functools.partial(shards, mesh.shape["row"], mesh.shape["col"])
    return jax.shard_map(body, mesh=mesh, in_specs=in_specs, out_specs=out_specs, check_vma=False)
```

time: 348 us -> 135 us (0.39)
  Pallas kernels: 0 us -> 135 us
  blocking collectives: 110 us -> 0 us
  other arithmetic: 91.3 us -> 0 us
  matrix products: 80 us -> 0 us
  waiting for transfers between devices: 28.6 us -> 0 us
  local copies, waits for them, and re-layouts: 21.2 us -> 0.01 us
  between operations: 14.2 us -> 0.69 us
    pallas_call x0 -> x4, Pallas kernels: none -> 135 us  [the longest x1 61.9 us: shards(): pl.pallas_call(squares_kernel, out_shape=[pltpu.VMEM((a.shape[0], 1, a.sh...]
    all_gather x4 -> x0, blocking collectives: 110 us -> none  [the longest x1 73.3 us: shards(): lax.all_gather(outer_left, 'col', axis=2, tiled=True)]
    another operation x5 -> x0, other arithmetic: 90.5 us -> none  [shards(): return (jnp.stack(inner_outputs), jnp.stack(outer_outputs))]
    dot_general x8 -> x0, matrix products: 80 us -> none  [combine_tile(): jnp.einsum('...ik,...kj->...ij', left, right, preferred_element_type=jnp....]
    psum x1 -> x0, waiting for transfers between devices: 28.6 us -> none  [merge_layer(): inner_totals, outer_totals = lax.psum((inner_squares, outer_squares), 'row')]
    unnamed x23 -> x4, local copies, waits for them, and re-layouts: 13.8 us -> 0.01 us
    slice x3 -> x0, local copies, waits for them, and re-layouts: 7.44 us -> none  [the longest x1 6.69 us: shards(): outer_rows[layer_index]]
  transfers between devices with their start and end apart: 1 -> 0, of which waited for: 1 -> 0; matrix products, arithmetic and copies ran while one was open for 0% -> 0% of each run, Pallas kernels for 0% -> 0%
where the time goes in v1:
time: 135 us
  Pallas kernels  135 us (100%)
    pallas_call x1, Pallas kernels, shards(): pl.pallas_call(squares_kernel, out_shape=[pltpu.VMEM((a.shape[0], 1, a.sh...  61.9 us
    pallas_call x1, Pallas kernels, shards(): pl.pallas_call(scale_kernel, out_shape=[jax.ShapeDtypeStruct(a.shape, bf1...  47.5 us
    pallas_call x1, Pallas kernels, shards(): pl.pallas_call(functools.partial(gather_kernel, rows, cols), out_shape=[p...  18.9 us
    pallas_call x1, Pallas kernels, shards(): pl.pallas_call(functools.partial(factor_kernel, rows), out_shape=[pltpu.V...  6.26 us

profile of v1, /device:TPU:1, one launch (start us, length us, event | category | flops | bytes accessed | tf_op | source)
XLA Modules:
  0.0 135.2 jit_solution(15243616959922291692)
XLA Ops:
  0.6 18.9 %gather.1 = (bf16[8,8,16,128]{3,2,1,0:T(8,128)(2,1)S(1)}, bf16[8,4,16,448]{3,2,1,0:T(8,128)(2,1)S(1)}, bf16[4,8,4,1792]{3,2,1,0:T(4,128)(2,1)S(1)}, bf16[4,4,4,5...) custom-call(bf16[8,16,128]{2,1,0:T(8,128)(2,1)} %bitcast.24, ...), custom_call_target="tpu_custom_call" | custom-call | tf_op jit(solution)/shard_map/gather/pallas_call | solution.py:224
  19.6 0.0 copy-start
  19.6 0.0 copy-start.1
  19.6 61.9 %squares.1 = (f32[8,1,1792]{2,1,0:T(1,128)S(1)}, f32[4,1,512]{2,1,0:T(1,128)S(1)}) custom-call(bf16[8,8,16,128]{3,2,1,0:T(8,128)(2,1)S(1)} %get-tuple-element.14.gil, bf16[8,4,16,448]{3,2,1,0:T(8,128)(2,1)S(1)} %get-tuple-element.15.gol, bf16[4,8,4,1792]{3,2,1,0:T(4,128)(2,1)S(1)} %get-tuple-element.16.gir, ...), custom_call_target="tpu_custom_call" | custom-call | tf_op jit(solution)/shard_map/squares/pallas_call | solution.py:247
  81.5 0.0 copy-done
  81.5 0.0 copy-done.1
  81.5 6.3 %factor.1 = (f32[8,1,1792]{2,1,0:T(1,128)S(1)}, f32[4,1,512]{2,1,0:T(1,128)S(1)}) custom-call(f32[8,1,1792]{2,1,0:T(1,128)S(1)} %get-tuple-element.20.sin, f32[4,1,512]{2,1,0:T(1,128)S(1)} %get-tuple-element.21.sout, f32[4,2,1792]{2,1,0:T(2,128)S(1)} %bitcast.19, f32[4,1,512]{2,1,0:T(1,128)S(1)} %copy-done.1), custom_call_target="tpu_custom_call" | custom-call | tf_op jit(solution)/shard_map/factor/pallas_call | solution.py:257
  87.8 47.5 %scale.1 = (bf16[8,1024,1792]{2,1,0:T(8,128)(2,1)}, bf16[4,3584,512]{2,1,0:T(8,128)(2,1)}) custom-call(bf16[8,8,16,128]{3,2,1,0:T(8,128)(2,1)S(1)} %get-tuple-element.14.gil, bf16[8,4,16,448]{3,2,1,0:T(8,128)(2,1)S(1)} %get-tuple-element.15.gol, bf16[4,8,4,1792]{3,2,1,0:T(4,128)(2,1)S(1)} %get-tuple-element.16.gir, ...), custom_call_target="tpu_custom_call" | custom-call | tf_op jit(solution)/shard_map/scale/pallas_call | solution.py:267
Async XLA Ops:
  19.6 61.9 %copy-start = (f32[4,1,2,1792]{3,2,1,0:T(2,128)S(1)}, f32[4,1,2,1792]{3,2,1,0:T(2,128)}, u32[]{:S(2)}) copy-start(f32[4,1,2,1792]{3,2,1,0:T(2,128)} %param.11) | copy-start | bytes 172036
  19.6 61.9 %copy-start.1 = (f32[4,1,512]{2,1,0:T(1,128)S(1)}, f32[4,1,512]{2,1,0:T(1,128)}, u32[]{:S(2)}) copy-start(f32[4,1,512]{2,1,0:T(1,128)} %mout.1) | copy-start | bytes 24580

commit v2 on v1

--- a/solution.py
+++ b/solution.py
@@ -12,7 +12,9 @@
 ANY = pl.BlockSpec(memory_space=pl.ANY)
 VMEM = pl.BlockSpec(memory_space=pltpu.VMEM)
 GRANT = 18 << 20
-SLOTS, PIECES = 4, 4
+SLOTS, PIECES = 4, 2
+WIDTHS = (256, 128)
+HEIGHTS = (512, 896, 256, 128, 64, 32, 16)
 
 
 def peers_of(axis, n):
@@ -93,8 +95,8 @@
 
 
 def tiles(rows, cols):
-    width = 256 if cols % 256 == 0 else 128 if cols % 128 == 0 else cols
-    height = next(h for h in (256, 128, 64, 32, 16) if rows % h == 0)
+    width = next((w for w in WIDTHS if cols % w == 0), cols)
+    height = next(h for h in HEIGHTS if rows % h == 0)
     return height, width
 
 
@@ -115,7 +117,7 @@
                 full = base[t, span, part].astype(jnp.float32) + delta
                 return total + jnp.sum((full * full).reshape(height // 8, 8, width), axis=0)
 
-            total = lax.fori_loop(0, rows // height, add, jnp.zeros((8, width), jnp.float32))
+            total = lax.fori_loop(0, rows // height, add, jnp.zeros((8, width), jnp.float32), unroll=True)
             acc[:, part] = total
         out[t] = jnp.sum(acc[...], axis=0, keepdims=True)
 
@@ -190,7 +192,7 @@
                     stage[slot, local, part] = merged.reshape(height, width).astype(jnp.bfloat16)
                     return carry
 
-                lax.fori_loop(0, chunk // height, merge, 0)
+                lax.fori_loop(0, chunk // height, merge, 0, unroll=True)
             store(step).start()
 
     return [store(step) for step in range(count * pieces - slots, count * pieces)]

time: 135 us -> 59.2 us (0.44)
  Pallas kernels: 135 us -> 58.4 us
    pallas_call x1, Pallas kernels: 61.9 us -> 14.9 us  [shards(): pl.pallas_call(squares_kernel, out_shape=[pltpu.VMEM((a.shape[0], 1, a.sh...]
    pallas_call x1, Pallas kernels: 47.5 us -> 18.2 us  [shards(): pl.pallas_call(scale_kernel, out_shape=[jax.ShapeDtypeStruct(a.shape, bf1...]
where the time goes in v2:
time: 59.2 us; the launch traced here: 59.1 us
  Pallas kernels  58.4 us (99%)
  between operations  0.68 us (1%)
    pallas_call x1, Pallas kernels, shards(): pl.pallas_call(functools.partial(gather_kernel, rows, cols), out_shape=[p...  18.9 us
    pallas_call x1, Pallas kernels, shards(): pl.pallas_call(scale_kernel, out_shape=[jax.ShapeDtypeStruct(a.shape, bf1...  18.2 us
    pallas_call x1, Pallas kernels, shards(): pl.pallas_call(squares_kernel, out_shape=[pltpu.VMEM((a.shape[0], 1, a.sh...  14.9 us
    pallas_call x1, Pallas kernels, shards(): pl.pallas_call(functools.partial(factor_kernel, rows), out_shape=[pltpu.V...  6.26 us

profile of v2, /device:TPU:1, one launch (start us, length us, event | category | flops | bytes accessed | tf_op | source)
XLA Modules:
  0.0 59.1 jit_solution(5620739818494543863)
XLA Ops:
  0.6 18.9 %gather.1 = (bf16[8,8,16,128]{3,2,1,0:T(8,128)(2,1)S(1)}, bf16[8,4,16,448]{3,2,1,0:T(8,128)(2,1)S(1)}, bf16[4,8,4,1792]{3,2,1,0:T(4,128)(2,1)S(1)}, bf16[4,4,4,5...) custom-call(bf16[8,16,128]{2,1,0:T(8,128)(2,1)} %bitcast.24, ...), custom_call_target="tpu_custom_call" | custom-call | tf_op jit(solution)/shard_map/gather/pallas_call | solution.py:226
  19.6 0.0 copy-start
  19.6 0.0 copy-start.1
  19.6 14.9 %squares.1 = (f32[8,1,1792]{2,1,0:T(1,128)S(1)}, f32[4,1,512]{2,1,0:T(1,128)S(1)}) custom-call(bf16[8,8,16,128]{3,2,1,0:T(8,128)(2,1)S(1)} %get-tuple-element.14.gil, bf16[8,4,16,448]{3,2,1,0:T(8,128)(2,1)S(1)} %get-tuple-element.15.gol, bf16[4,8,4,1792]{3,2,1,0:T(4,128)(2,1)S(1)} %get-tuple-element.16.gir, ...), custom_call_target="tpu_custom_call" | custom-call | tf_op jit(solution)/shard_map/squares/pallas_call | solution.py:249
  34.5 0.0 copy-done
  34.5 0.0 copy-done.1
  34.6 6.3 %factor.1 = (f32[8,1,1792]{2,1,0:T(1,128)S(1)}, f32[4,1,512]{2,1,0:T(1,128)S(1)}) custom-call(f32[8,1,1792]{2,1,0:T(1,128)S(1)} %get-tuple-element.20.sin, f32[4,1,512]{2,1,0:T(1,128)S(1)} %get-tuple-element.21.sout, f32[4,2,1792]{2,1,0:T(2,128)S(1)} %bitcast.19, f32[4,1,512]{2,1,0:T(1,128)S(1)} %copy-done.1), custom_call_target="tpu_custom_call" | custom-call | tf_op jit(solution)/shard_map/factor/pallas_call | solution.py:259
  40.8 18.2 %scale.1 = (bf16[8,1024,1792]{2,1,0:T(8,128)(2,1)}, bf16[4,3584,512]{2,1,0:T(8,128)(2,1)}) custom-call(bf16[8,8,16,128]{3,2,1,0:T(8,128)(2,1)S(1)} %get-tuple-element.14.gil, bf16[8,4,16,448]{3,2,1,0:T(8,128)(2,1)S(1)} %get-tuple-element.15.gol, bf16[4,8,4,1792]{3,2,1,0:T(4,128)(2,1)S(1)} %get-tuple-element.16.gir, ...), custom_call_target="tpu_custom_call" | custom-call | tf_op jit(solution)/shard_map/scale/pallas_call | solution.py:269
Async XLA Ops:
  19.6 15.0 %copy-start = (f32[4,1,2,1792]{3,2,1,0:T(2,128)S(1)}, f32[4,1,2,1792]{3,2,1,0:T(2,128)}, u32[]{:S(2)}) copy-start(f32[4,1,2,1792]{3,2,1,0:T(2,128)} %param.11) | copy-start | bytes 172036
  19.6 15.0 %copy-start.1 = (f32[4,1,512]{2,1,0:T(1,128)S(1)}, f32[4,1,512]{2,1,0:T(1,128)}, u32[]{:S(2)}) copy-start(f32[4,1,512]{2,1,0:T(1,128)} %mout.1) | copy-start | bytes 24580
